TPU v7x, 32 devices: a whole 2x2x4 slice. The times are simulated.
32 devices in a mesh: dp: 8 (over z, y), mp: 4 (over x, core).
Axes of the slice: x: 2, y: 2, z: 4, core: 2. Of those that a mesh axis runs over, the one named last changes fastest.
Arguments:
- documents: bfloat16 [16384, 1024], P('dp', 'mp'), may hold values from -6 to 6
- assign: int32 [16384], P('dp'), may hold values from 0 to 4095, as said below
- quality: float32 [16384], P('dp'), may hold values from 0.1 to 1
- centroids: bfloat16 [4096, 1024], P('mp'), may hold values from -6 to 6
Outputs:
- distances: float32 [16384], P('dp')
- new_centroids: bfloat16 [4096, 1024], P('dp', 'mp')
- cluster_quality: float32 [4096], P('dp')
- inertia: float32 [], replicated
Inputs may be any that keep to these rules, and one draw needn't show every extreme that they name: `assign`: call the clusters o * 512 to (o + 1) * 512 - 1 those of owner o. Among each run of 2048 documents held by one index of dp, at most 512 have clusters of any one owner, and one owner, the same for every index, gets exactly 512 of them from every index.
All inputs are finite; a program needn't handle non-finite values.
Results may differ from a plain program's by a relative error of at most 0.0044.
Values may be sent and summed in bfloat16 or wider, within the bound.
A program may use at most 64 MiB of HBM per device.

v0:
```python
import jax
import jax.numpy as jnp
from jax import lax
from jax.sharding import PartitionSpec as P

D = 1024


def per_device(documents, assign, quality, centroids):
    rows = documents.shape[0]
    width = documents.shape[1]
    feature_cents = lax.all_to_all(centroids, "mp", split_axis=1, concat_axis=0, tiled=True)
    clusters = feature_cents.shape[0]
    block = min(512, rows)
    labels = lax.broadcasted_iota(jnp.int32, (1, clusters), 1)
    weight_all = quality.astype(jnp.bfloat16)
    sums = jnp.zeros((clusters, width), jnp.float32)
    counts = jnp.zeros((clusters,), jnp.float32)
    mass = jnp.zeros((clusters,), jnp.float32)
    partial_list = []
    for start in range(0, rows, block):
        docs_blk = documents[start : start + block]
        onehot = (assign[start : start + block][:, None] == labels).astype(jnp.bfloat16)
        picked = jnp.dot(onehot, feature_cents, preferred_element_type=jnp.float32)
        diff = docs_blk.astype(jnp.float32) - picked
        partial_list.append(jnp.sum(diff * diff, axis=1))
        weighted = onehot * weight_all[start : start + block][:, None]
        sums = sums + lax.dot_general(
            weighted, docs_blk, (((0,), (0,)), ((), ())), preferred_element_type=jnp.float32
        )
        counts = counts + jnp.sum(onehot.astype(jnp.float32), axis=0)
        mass = mass + jnp.sum(weighted.astype(jnp.float32), axis=0)
    partial_value = jnp.concatenate(partial_list, axis=0)
    distances = lax.psum(partial_value, "mp") / D
    total_docs = rows * lax.axis_size("dp")
    inertia = lax.psum(jnp.sum(distances), "dp") / total_docs
    owners_count = lax.axis_size("dp")
    share = clusters // owners_count
    first = lax.axis_index("dp") * share
    own_sums, own_counts, own_mass = (
        lax.psum_scatter(sums, "dp", scatter_dimension=0, tiled=True),
        lax.psum_scatter(counts, "dp", scatter_dimension=0, tiled=True),
        lax.psum_scatter(mass, "dp", scatter_dimension=0, tiled=True),
    )
    old_rows = lax.dynamic_slice_in_dim(feature_cents, first, share, 0).astype(jnp.float32)
    new_centroids = ((own_sums + old_rows) / (own_mass + 1.0)[:, None]).astype(jnp.bfloat16)
    cluster_quality = own_mass / (own_counts + 1.0)
    return (distances, new_centroids, cluster_quality, inertia)


def solution(mesh):
    return jax.shard_map(
        per_device,
        mesh=mesh,
        in_specs=(P("dp", "mp"), P("dp"), P("dp"), P("mp", None)),
        out_specs=(P("dp"), P("dp", "mp"), P("dp"), P()),
        check_vma=False,
    )
```

profile of v0, /device:TPU:0, one launch (start us, length us, event | category | flops | bytes accessed | tf_op | source)
XLA Modules:
  0.0 120.2 jit_solution(4028343707287706201)
XLA Ops:
  7.2 0.0 reduce-scatter.2.cloned.1.call-start
  7.2 0.8 fusion.56
  8.0 0.7 convert_element_type.61
  8.7 0.0 copy-start.1
  8.7 2.6 %fusion.12 = f32[4096,256]{1,0:T(8,128)S(1)} fusion(s32[512]{0:T(512)S(1)} %get-tuple-element.23, bf16[512]{0:T(512)(128)(2,1)S(1)} %get-tuple-element.30, bf16[2048,256]{1,0:T(8,128)(2,1)} %param.4), kind=kOutput, calls=%fused_computation.27 | convolution fusion | flops 1077936128 | bytes 4459520 | tf_op jit(solution)/shard_map/dot_general | solution.py:28
  11.3 0.0 copy-done.1
  11.3 1.8 %convolution_add_fusion.2 = f32[4096,256]{1,0:T(8,128)S(1)} fusion(f32[4096,256]{1,0:T(8,128)S(1)} %fusion.12, s32[512]{0:T(512)S(1)} %get-tuple-element.24, bf16[512]{0:T(512)(128)(2,1)S(1)} %get-tuple-element.29, bf16[2048,256]{1,0:T(8,128)(2,1)S(1)} %copy-done.1), kind=kOutput, calls=%fused_computation.26 | convolution fusion | flops 1078984704 | bytes 8653824 | tf_op jit(solution)/shard_map/dot_general | solution.py:28
  13.1 1.8 %convolution_add_fusion.1 = f32[4096,256]{1,0:T(8,128)S(1)} fusion(f32[4096,256]{1,0:T(8,128)S(1)} %convolution_add_fusion.2, s32[512]{0:T(512)S(1)} %get-tuple-element.26, bf16[512]{0:T(512)(128)(2,1)S(1)} %get-tuple-element.28, bf16[2048,256]{1,0:T(8,128)(2,1)S(1)} %copy-done.1), kind=kOutput, calls=%fused_computation.25 | convolution fusion | flops 1078984704 | bytes 8653824 | tf_op jit(solution)/shard_map/dot_general | solution.py:28
  14.8 3.7 %convolution_add_fusion = f32[4096,256]{1,0:T(8,128)} fusion(f32[4096,256]{1,0:T(8,128)S(1)} %convolution_add_fusion.1, s32[512]{0:T(512)S(1)} %get-tuple-element.25, bf16[512]{0:T(512)(128)(2,1)S(1)} %get-tuple-element.27, bf16[2048,256]{1,0:T(8,128)(2,1)S(1)} %copy-done.1), kind=kOutput, calls=%fused_computation.24 | convolution fusion | flops 1078984704 | bytes 8653824 | tf_op jit(solution)/shard_map/dot_general | solution.py:28
  18.5 0.0 copy-start
  18.5 0.0 reduce-scatter.2.cloned.1.call-update
  18.6 1.6 %copy-done = bf16[1024,1024]{1,0:T(8,128)(2,1)S(1)} copy-done((bf16[1024,1024]{1,0:T(8,128)(2,1)S(1)}, bf16[1024,1024]{1,0:T(8,128)(2,1)}, u32[]{:S(2)}) %copy-start) | copy-done | bytes 2097176
  20.1 1.5 %copy.29 = bf16[128,4,8,256]{3,2,0,1:T(8,128)(2,1)} copy(bf16[128,4,8,256]{3,2,1,0:T(8,128)(2,1)S(1)} %bitcast.17) | data formatting | bytes 4194304 | tf_op jit(solution)/shard_map/all_to_all | solution.py:12
  21.6 0.0 copy-start.2
  21.6 4.4 %all-to-all-start = ((bf16[1024,4,256]{2,0,1:T(8,128)(2,1)}), bf16[1024,4,256]{2,0,1:T(8,128)(2,1)S(1)}, u32[]{:S(2)}, u32[]{:S(2)}) async-start(bf16[1024,4,256]{2,0,1:T(8,128)(2,1)} %bitcast.11), calls=%async_computation | async-start | bytes 4194304 | tf_op jit(solution)/shard_map/all_to_all | solution.py:12
  26.0 0.9 fusion.55
  26.9 1.1 copy.26
  28.0 1.2 copy.25
  29.1 1.1 copy.24
  30.2 0.1 copy.23
  30.4 0.0 copy-done.2
  30.4 0.6 dynamic-slice
  31.6 4.3 %convert_reduce_fusion = (f32[4096]{0:T(1024)S(1)}, f32[4096]{0:T(1024)S(1)}, f32[4096]{0:T(1024)S(1)}, f32[4096]{0:T(1024)S(1)}) fusion(s32[512]{0:T(512)S(1)} %get-tuple-element.25, bf16[512]{0:T(512)(128)(2,1)S(1)} %get-tuple-element.27, bf16[512]{0:T(512)(128)(2,1)S(1)} %get-tuple-element.28, s32[512]{0:T(512)S(1)} %get-tuple-element.26), kind=kLoop, calls=%fused_computation | loop fusion | flops 29343744 | bytes 71680 | tf_op jit(solution)/shard_map/reduce_sum | solution.py:31
  35.9 4.5 %convert_reduce_fusion.2 = (f32[4096]{0:T(1024)S(1)}, f32[4096]{0:T(1024)S(1)}, f32[4096]{0:T(1024)S(1)}, f32[4096]{0:T(1024)S(1)}) fusion(s32[512]{0:T(512)S(1)} %get-tuple-element.24, bf16[512]{0:T(512)(128)(2,1)S(1)} %get-tuple-element.29, bf16[512]{0:T(512)(128)(2,1)S(1)} %get-tuple-element.30, s32[512]{0:T(512)S(1)} %get-tuple-element.23), kind=kLoop, calls=%fused_computation.2 | loop fusion | flops 29343744 | bytes 71680 | tf_op jit(solution)/shard_map/reduce_sum | solution.py:31
  40.5 11.3 %all-to-all-done = bf16[1024,4,256]{2,0,1:T(8,128)(2,1)S(1)} async-done(((bf16[1024,4,256]{2,0,1:T(8,128)(2,1)}), bf16[1024,4,256]{2,0,1:T(8,128)(2,1)S(1)}, u32[]{:S(2)}, u32[]{:S(2)}) %all-to-all-start) | async-done | bytes 2097184 | tf_op jit(solution)/shard_map/all_to_all | solution.py:12
  51.8 2.1 %fusion.41 = f32[512]{0:T(512)S(1)} fusion(bf16[4096,256]{1,0:T(8,128)(2,1)S(1)} %bitcast.12, s32[512]{0:T(512)S(1)} %get-tuple-element.25, bf16[512,256]{0,1:T(8,128)(2,1)S(1)} %copy.26), kind=kOutput, calls=%fused_computation.53 | convolution fusion | flops 1076362752 | bytes 2363392 | tf_op jit(solution)/shard_map/dot_general | solution.py:24
  54.0 2.1 %fusion.42 = f32[512]{0:T(512)S(1)} fusion(bf16[4096,256]{1,0:T(8,128)(2,1)S(1)} %bitcast.13, s32[512]{0:T(512)S(1)} %get-tuple-element.26, bf16[512,256]{0,1:T(8,128)(2,1)S(1)} %copy.25), kind=kOutput, calls=%fused_computation.54 | convolution fusion | flops 1076362752 | bytes 2363392 | tf_op jit(solution)/shard_map/dot_general | solution.py:24
  56.1 2.1 %fusion.43 = f32[512]{0:T(512)S(1)} fusion(bf16[4096,256]{1,0:T(8,128)(2,1)S(1)} %bitcast.14, s32[512]{0:T(512)S(1)} %get-tuple-element.24, bf16[512,256]{0,1:T(8,128)(2,1)S(1)} %copy.24), kind=kOutput, calls=%fused_computation.55 | convolution fusion | flops 1076362752 | bytes 2363392 | tf_op jit(solution)/shard_map/dot_general | solution.py:24
  58.2 2.1 %fusion.44 = f32[512]{0:T(512)S(1)} fusion(bf16[4096,256]{1,0:T(8,128)(2,1)S(1)} %bitcast.15, s32[512]{0:T(512)S(1)} %get-tuple-element.23, bf16[512,256]{0,1:T(8,128)(2,1)S(1)} %copy.23), kind=kOutput, calls=%fused_computation.56 | convolution fusion | flops 1076362752 | bytes 2363392 | tf_op jit(solution)/shard_map/dot_general | solution.py:24
  60.4 6.2 %psum.14 = f32[2048]{0:T(1024)S(1)} all-reduce(f32[2048]{0:T(1024)S(1)} %pad_maximum_fusion), channel_id=1, replica_groups=mesh['dp'=8,'mp'=4] {'mp'}, use_global_device_ids=true, to_apply=%region_4.0 | all-reduce | flops 2048 | bytes 16384 | tf_op jit(solution)/shard_map/psum | solution.py:34
  66.6 1.2 fusion.54
  67.8 40.5 %all-reduce.2 = (f32[4096]{0:T(1024)S(1)}, f32[4096]{0:T(1024)S(1)}, f32[]{:T(128)}) all-reduce(f32[4096]{0:T(1024)S(1)} %add_add_fusion.1, f32[4096]{0:T(1024)S(1)} %add_add_fusion, f32[]{:T(128)} %get-tuple-element.15), channel_id=3, replica_groups=mesh['dp'=8,'mp'=4] {'dp'}, use_global_device_ids=true, to_apply=%region_10.0.clone | all-reduce | flops 8193 | bytes 65544
  108.9 0.7 fusion.45
  109.6 0.7 reduce-scatter.2.cloned.1.call-done
  110.3 1.9 %divide_convert_fusion = bf16[512,256]{1,0:T(8,128)(2,1)} fusion(f32[512,256]{1,0:T(8,128)} %reduce-scatter.2.cloned.1.call-done, f32[512]{0:T(512)S(1)} %get-tuple-element.22, bf16[4096,256]{1,0:T(8,128)(2,1)S(1)} %bitcast.16, s32[]{:T(128)S(6)} %select_n.3), kind=kLoop, calls=%fused_computation.57 | loop fusion | flops 524288 | bytes 1050628 | tf_op jit(solution)/shard_map/convert_element_type | solution.py:46
  (4 shorter events, 0.0 us)
Async XLA Ops:
  7.2 103.1 %reduce-scatter.2.cloned.1.call-start = ((), (), s32[]{:S(2)}) async-start(), calls=%async_computation.2 | async-start | bytes 4718592 | tf_op jit(solution)/shard_map/reduce_scatter | solution.py:41
  8.7 2.6 %copy-start.1 = (bf16[2048,256]{1,0:T(8,128)(2,1)S(1)}, bf16[2048,256]{1,0:T(8,128)(2,1)}, u32[]{:S(2)}) copy-start(bf16[2048,256]{1,0:T(8,128)(2,1)} %param.4) | copy-start | bytes 3145732
  18.5 1.6 %copy-start = (bf16[1024,1024]{1,0:T(8,128)(2,1)S(1)}, bf16[1024,1024]{1,0:T(8,128)(2,1)}, u32[]{:S(2)}) copy-start(bf16[1024,1024]{1,0:T(8,128)(2,1)} %param.7) | copy-start | bytes 6291460
  21.6 8.8 %copy-start.2 = (u32[32]{0:T(128)S(1)}, u32[32]{0:T(128)}, u32[]{:S(2)}) copy-start(u32[32]{0:T(128)} %constant.29) | copy-start | bytes 388
  21.6 30.2 %all-to-all-start = ((bf16[1024,4,256]{2,0,1:T(8,128)(2,1)}), bf16[1024,4,256]{2,0,1:T(8,128)(2,1)S(1)}, u32[]{:S(2)}, u32[]{:S(2)}) async-start(bf16[1024,4,256]{2,0,1:T(8,128)(2,1)} %bitcast.11), calls=%async_computation | async-start | bytes 4194304 | tf_op jit(solution)/shard_map/all_to_all | solution.py:12
Sparse Core Ops, SparseCore 0:
  18.7 91.5 reduce-scatter.1
where the time goes:
time: 121 us; the launch traced here: 120 us
  blocking collectives  46.6 us (39%)
  matrix products  18.4 us (15%)
  between operations  16.6 us (14%)
  other arithmetic  13.3 us (11%)
  waiting for transfers between devices  12.1 us (10%)
  local copies, waits for them, and re-layouts  8.8 us (7%)
  starting transfers between devices  4.41 us (4%)
    unnamed x1, blocking collectives  40.5 us
    all_to_all x1, waiting for transfers between devices, per_device(): lax.all_to_all(centroids, 'mp', split_axis=1, concat_axis=0, tiled=True)  11.3 us
    dot_general x4, matrix products, per_device(): lax.dot_general(weighted, docs_blk, (((0,), (0,)), ((), ())), preferred_e...  9.8 us
    reduce_sum x2, other arithmetic, per_device(): counts = counts + jnp.sum(onehot.astype(jnp.float32), axis=0)  8.81 us
    dot_general x4, matrix products, per_device(): picked = jnp.dot(onehot, feature_cents, preferred_element_type=jnp.float32)  8.57 us
    unnamed x12, local copies, waits for them, and re-layouts  6.55 us
    psum x1, blocking collectives, per_device(): distances = lax.psum(partial_value, 'mp') / D  6.17 us
    all_to_all x1, starting transfers between devices, per_device(): lax.all_to_all(centroids, 'mp', split_axis=1, concat_axis=0, tiled=True)  4.37 us
  transfers between devices with their start and end apart: 2, of which 2 were waited for; matrix products, arithmetic and copies ran while one was open for 21% of the time, Pallas kernels for 0%

commit v1 on v0

v1 whole, which is shorter than its diff:
```python
import functools

import jax
import jax.numpy as jnp
from jax import lax
from jax.experimental import pallas as pl
from jax.experimental.pallas import tpu as pltpu
from jax.sharding import PartitionSpec as P

MESH = pl.DeviceIdType.MESH
LANES = 128
CHUNKS = 4


def kernel(
    n_dp, n_mp, assign_ref, quality_ref, docs_ref, cents_ref,
    dist_ref, new_ref, cq_ref, inertia_ref,
    fc, acc, acol, own, ysend, ybuf, zsend, zbuf, ag, qg, dbuf, ibuf, isend,
    a_ss, a_rs, a_ls, g_ss, g_rs, y_ss, y_rs, z_ss, z_rs, d_ss, d_rs, i_ss, i_rs,
):
    f32, bf16 = jnp.float32, jnp.bfloat16
    dp, mp = lax.axis_index("dp"), lax.axis_index("mp")
    n_hi = n_dp // 2
    hi, lo = dp // 2, dp % 2
    rows, width = docs_ref.shape
    depth = cents_ref.shape[0]
    share = new_ref.shape[0]
    nb = rows // LANES
    clen = depth // CHUNKS

    barrier = pltpu.get_barrier_semaphore()
    for s in range(1, n_mp):
        pl.semaphore_signal(barrier, inc=1, device_id={"mp": (mp + s) % n_mp}, device_id_type=MESH)

    @pl.loop(1, n_dp)
    def _(s):
        pl.semaphore_signal(barrier, inc=1, device_id={"dp": (dp + s) % n_dp}, device_id_type=MESH)

    pl.semaphore_wait(barrier, n_mp - 1 + n_dp - 1)

    def cent_copy(peer, slot, c):
        cols = pl.ds(pl.multiple_of(peer * width, LANES), width)
        return pltpu.make_async_remote_copy(
            src_ref=cents_ref.at[pl.ds(c * clen, clen), cols],
            dst_ref=fc.at[slot, pl.ds(c * clen, clen), :],
            send_sem=a_ss.at[peer, c],
            recv_sem=a_rs.at[slot, c],
            device_id={"mp": peer},
            device_id_type=MESH,
        )

    near = mp + 1 - 2 * (mp % 2)
    fars = [(d + 2 * s) % n_mp for s in range(1, n_mp // 2) for d in (mp, near)]
    peers = [near] + fars
    for c in range(CHUNKS):
        for peer in fars:
            cent_copy(peer, mp, c).start()
    for c in range(CHUNKS):
        cent_copy(near, mp, c).start()
    mine = pltpu.make_async_copy(
        cents_ref.at[:, pl.ds(pl.multiple_of(mp * width, LANES), width)], fc.at[mp], a_ls
    )
    mine.start()

    def gather_copies(peer, slot):
        return [
            pltpu.make_async_remote_copy(
                src_ref=src, dst_ref=dst.at[slot], send_sem=g_ss.at[i, peer],
                recv_sem=g_rs.at[i, slot], device_id={"dp": peer}, device_id_type=MESH,
            )
            for i, (src, dst) in enumerate(((assign_ref, ag), (quality_ref, qg)))
        ]

    @pl.loop(1, n_dp)
    def _(s):
        for copy in gather_copies((dp + s) % n_dp, dp):
            copy.start()

    row_iota = lax.broadcasted_iota(jnp.int32, (share, LANES), 0)

    def partial(owner):
        base = owner * share
        pieces = []
        for b in range(nb):
            hit = (assign_ref[pl.ds(b, 1), :] - base) == row_iota
            pieces.append(jnp.where(hit, quality_ref[pl.ds(b, 1), :], 0.0).astype(bf16))
        weighted = jnp.concatenate(pieces, axis=1)
        return jnp.dot(weighted, docs_ref[...], preferred_element_type=f32)

    def y_copy(h):
        return pltpu.make_async_remote_copy(
            src_ref=ysend.at[h], dst_ref=ybuf.at[h], send_sem=y_ss.at[h], recv_sem=y_rs.at[h],
            device_id={"dp": hi * 2 + 1 - lo}, device_id_type=MESH,
        )

    @pl.loop(0, n_hi)
    def _(k):
        h = (hi + 1 + k) % n_hi
        ysend[h] = partial(h * 2 + 1 - lo).astype(bf16)
        y_copy(h).start()

    @pl.loop(0, n_hi)
    def _(k):
        h = (hi + 1 + k) % n_hi
        own[h] = partial(h * 2 + lo)

    def z_copy(h, slot):
        return pltpu.make_async_remote_copy(
            src_ref=zsend.at[h], dst_ref=zbuf.at[slot], send_sem=z_ss.at[h], recv_sem=z_rs.at[slot],
            device_id={"dp": h * 2 + lo}, device_id_type=MESH,
        )

    def forward(k):
        h = (hi + 1 + k) % n_hi
        y_copy(h).wait_recv()
        zsend[h] = (own[h] + ybuf[h].astype(f32)).astype(bf16)
        z_copy(h, hi).start()

    for b in range(nb):
        ids = jnp.broadcast_to(assign_ref[pl.ds(b, 1), :].astype(f32), (LANES, LANES))
        acol[pl.ds(b * LANES, LANES), :] = ids.T

    tile = min(512, rows)

    def pick(src, start, size, first=False):
        base = (src * depth + start).astype(f32)

        @pl.loop(0, rows // tile)
        def _(t):
            at = pl.ds(pl.multiple_of(t * tile, tile), tile)
            ids = acol[at, :] - base
            lane = lax.broadcasted_iota(jnp.int32, (tile, LANES), 1)
            onehot = jnp.concatenate(
                [
                    jnp.where(ids == (lane + j * LANES).astype(f32), 1.0, 0.0).astype(bf16)
                    for j in range(size // LANES)
                ],
                axis=1,
            )
            got = jnp.dot(onehot, fc[src, pl.ds(start, size), :], preferred_element_type=f32)
            prior = docs_ref[at, :].astype(f32) if first else acc[at, :]
            acc[at, :] = prior - got

    mine.wait()
    pick(mp, 0, depth, first=True)
    forwards = n_hi - 1
    cut = [forwards * c // (CHUNKS - 1) for c in range(CHUNKS)]
    if CHUNKS > 1:
        pl.loop(cut[0], cut[1])(forward)
    for c in range(CHUNKS):
        cent_copy(near, near, c).wait_recv()
    pick(near, 0, depth)

    lane_len = min(LANES, share)
    groups = share // lane_len
    half = max(4, groups)
    ag[dp] = assign_ref[...]
    qg[dp] = quality_ref[...]

    def count(i, total):
        d = (dp + i) % n_dp

        @pl.when(i > 0)
        def _():
            for copy in gather_copies(d, d):
                copy.wait_recv()

        left, right = [], []
        part = lax.broadcasted_iota(jnp.int32, (2 * half, LANES), 0)
        low = lax.broadcasted_iota(jnp.int32, (lane_len, LANES), 0)
        for b in range(nb):
            ids = ag[d, pl.ds(b, 1), :] - dp * share
            upper = ids >> (lane_len.bit_length() - 1)
            lower = ids & (lane_len - 1)
            weight = jnp.where(part < half, 1.0, qg[d, pl.ds(b, 1), :])
            member = jnp.where(part < half, part, part - half) == upper
            left.append(jnp.where(member, weight, 0.0).astype(bf16))
            right.append(jnp.where(low == lower, 1.0, 0.0).astype(bf16))
        return total + lax.dot_general(
            jnp.concatenate(left, axis=1), jnp.concatenate(right, axis=1),
            (((1,), (1,)), ((), ())), preferred_element_type=f32,
        )

    totals = lax.fori_loop(0, n_dp, count, jnp.zeros((2 * half, lane_len), f32))
    counts, mass = totals[:groups], totals[half : half + groups]
    cq_ref[...] = mass / (counts + 1.0)

    for c in range(CHUNKS):
        for peer in fars:
            cent_copy(peer, peer, c).wait_recv()
            pick(peer, c * clen, clen)
        if c + 2 < CHUNKS:
            pl.loop(cut[c + 1], cut[c + 2])(forward)

    @pl.loop(0, nb)
    def _(b):
        diff = acc[pl.ds(pl.multiple_of(b * LANES, LANES), LANES), :]
        square = diff * diff
        folded = square[:, :LANES]
        for j in range(1, width // LANES):
            folded = folded + square[:, j * LANES : (j + 1) * LANES]
        dbuf[mp, pl.ds(b, 1), :] = jnp.sum(folded.T, axis=0, keepdims=True)

    def d_copy(peer, slot):
        return pltpu.make_async_remote_copy(
            src_ref=dbuf.at[mp], dst_ref=dbuf.at[slot], send_sem=d_ss.at[peer], recv_sem=d_rs.at[slot],
            device_id={"mp": peer}, device_id_type=MESH,
        )

    for peer in peers:
        d_copy(peer, mp).start()
    for peer in peers:
        d_copy(peer, peer).wait_recv()
    dist = dbuf[0]
    for s in range(1, n_mp):
        dist = dist + dbuf[s]
    dist = dist / (width * n_mp)
    dist_ref[...] = dist
    folded = dist[:8]
    for j in range(1, nb // 8):
        folded = folded + dist[j * 8 : (j + 1) * 8]
    isend[...] = folded

    def i_copy(peer, slot):
        return pltpu.make_async_remote_copy(
            src_ref=isend, dst_ref=ibuf.at[slot], send_sem=i_ss.at[peer], recv_sem=i_rs.at[slot],
            device_id={"dp": peer}, device_id_type=MESH,
        )

    @pl.loop(1, n_dp)
    def _(s):
        i_copy((dp + s) % n_dp, dp).start()

    ibuf[dp] = folded

    y_copy(hi).wait_recv()
    own[hi] = own[hi] + ybuf[hi].astype(f32)

    @pl.loop(1, n_hi)
    def _(s):
        h = (hi + s) % n_hi
        z_copy(h, h).wait_recv()
        own[hi] = own[hi] + zbuf[h].astype(f32)

    first = dp * share
    src, start = first // depth, first % depth
    for g in range(groups):
        column = jnp.broadcast_to(mass[g : g + 1, :], (LANES, lane_len)).T + 1.0
        column = jnp.concatenate([column] * (width // LANES), axis=1)
        at = pl.ds(g * lane_len, lane_len)
        old = fc[src, pl.ds(pl.multiple_of(start + g * lane_len, lane_len), lane_len), :].astype(f32)
        new_ref[at, :] = ((own[hi, at, :] + old) / column).astype(bf16)

    @pl.loop(1, n_dp)
    def _(s):
        d = (dp + s) % n_dp
        i_copy(d, d).wait_recv()

    total = lax.fori_loop(1, n_dp, lambda d, t: t + ibuf[d], ibuf[0])
    inertia_ref[0, 0] = jnp.sum(total) / (rows * n_dp)

    for peer in peers:
        d_copy(peer, mp).wait_send()
        for c in range(CHUNKS):
            cent_copy(peer, mp, c).wait_send()

    @pl.loop(1, n_dp)
    def _(s):
        d = (dp + s) % n_dp
        i_copy(d, dp).wait_send()
        for copy in gather_copies(d, dp):
            copy.wait_send()

    @pl.loop(0, n_hi)
    def _(h):
        y_copy(h).wait_send()

    @pl.loop(1, n_hi)
    def _(s):
        z_copy((hi + s) % n_hi, hi).wait_send()


def per_device(n_dp, n_mp, documents, assign, quality, centroids):
    rows, width = documents.shape
    depth = centroids.shape[0]
    share = depth * n_mp // n_dp
    nb = rows // LANES
    n_hi = n_dp // 2
    lane_len = min(LANES, share)
    f32, bf16 = jnp.float32, jnp.bfloat16
    vmem = pl.BlockSpec(memory_space=pltpu.VMEM)
    dma = pltpu.SemaphoreType.DMA
    dist, new, cq, inertia = pl.pallas_call(
        functools.partial(kernel, n_dp, n_mp),
        out_shape=(
            jax.ShapeDtypeStruct((nb, LANES), f32),
            jax.ShapeDtypeStruct((share, width), bf16),
            jax.ShapeDtypeStruct((share // lane_len, lane_len), f32),
            jax.ShapeDtypeStruct((1, 1), f32),
        ),
        in_specs=[vmem, vmem, vmem, pl.BlockSpec(memory_space=pl.ANY)],
        out_specs=(vmem, vmem, vmem, pl.BlockSpec(memory_space=pltpu.SMEM)),
        scratch_shapes=[
            pltpu.VMEM((n_mp, depth, width), bf16),
            pltpu.VMEM((rows, width), f32),
            pltpu.VMEM((rows, LANES), f32),
            pltpu.VMEM((n_hi, share, width), f32),
            pltpu.VMEM((n_hi, share, width), bf16),
            pltpu.VMEM((n_hi, share, width), bf16),
            pltpu.VMEM((n_hi, share, width), bf16),
            pltpu.VMEM((n_hi, share, width), bf16),
            pltpu.VMEM((n_dp, nb, LANES), jnp.int32),
            pltpu.VMEM((n_dp, nb, LANES), f32),
            pltpu.VMEM((n_mp, nb, LANES), f32),
            pltpu.VMEM((n_dp, 8, LANES), f32),
            pltpu.VMEM((8, LANES), f32),
            dma((n_mp, CHUNKS)), dma((n_mp, CHUNKS)), dma,
            dma((2, n_dp)), dma((2, n_dp)),
            dma((n_hi,)), dma((n_hi,)),
            dma((n_hi,)), dma((n_hi,)),
            dma((n_mp,)), dma((n_mp,)),
            dma((n_dp,)), dma((n_dp,)),
        ],
        compiler_params=pltpu.CompilerParams(
            collective_id=0, has_side_effects=True, vmem_limit_bytes=48 * 2**20
        ),
    )(assign.reshape(nb, LANES), quality.reshape(nb, LANES), documents, centroids)
    return dist.reshape(rows), new, cq.reshape(share), inertia.reshape(())


def solution(mesh):
    return jax.shard_map(
        functools.partial(per_device, mesh.shape["dp"], mesh.shape["mp"]),
        mesh=mesh,
        in_specs=(P("dp", "mp"), P("dp"), P("dp"), P("mp", None)),
        out_specs=(P("dp"), P("dp", "mp"), P("dp"), P()),
        check_vma=False,
    )
```

time: 121 us -> 50.7 us (0.42)
  blocking collectives: 46.6 us -> 0 us
  Pallas kernels: 0 us -> 41.9 us
  matrix products: 18.4 us -> 0 us
  between operations: 16.6 us -> 2.4 us
  other arithmetic: 13.3 us -> 0 us
  waiting for transfers between devices: 12.1 us -> 0 us
  starting transfers between devices: 4.41 us -> 0 us
  local copies, waits for them, and re-layouts: 8.8 us -> 6.08 us
    pallas_call x0 -> x1, Pallas kernels: none -> 41.9 us  [per_device(): pl.pallas_call(functools.partial(kernel, n_dp, n_mp), out_shape=(jax.Shap...]
    unnamed x1 -> x0, blocking collectives: 40.5 us -> none
    dot_general x8 -> x0, matrix products: 18.4 us -> none  [the longest x4 9.8 us: per_device(): lax.dot_general(weighted, docs_blk, (((0,), (0,)), ((), ())), preferred_e...]
    all_to_all x1 -> x0, waiting for transfers between devices: 11.3 us -> none  [per_device(): lax.all_to_all(centroids, 'mp', split_axis=1, concat_axis=0, tiled=True)]
    reduce_sum x3 -> x0, other arithmetic: 10 us -> none  [the longest x2 8.81 us: per_device(): counts = counts + jnp.sum(onehot.astype(jnp.float32), axis=0)]
    psum x1 -> x0, blocking collectives: 6.17 us -> none  [per_device(): distances = lax.psum(partial_value, 'mp') / D]
    all_to_all x1 -> x0, starting transfers between devices: 4.37 us -> none  [per_device(): lax.all_to_all(centroids, 'mp', split_axis=1, concat_axis=0, tiled=True)]
    convert_element_type x2 -> x0, other arithmetic: 2.58 us -> none  [the longest x1 1.88 us: per_device(): ((own_sums + old_rows) / (own_mass + 1.0)[:, None]).astype(jnp.bfloat16)]
  transfers between devices with their start and end apart: 2 -> 0, of which waited for: 2 -> 0; matrix products, arithmetic and copies ran while one was open for 21% -> 0% of each run, Pallas kernels for 0% -> 0%
where the time goes in v1:
time: 50.7 us; the launch traced here: 50.4 us
  Pallas kernels  41.9 us (83%)
  local copies, waits for them, and re-layouts  6.08 us (12%)
  between operations  2.4 us (5%)
    pallas_call x1, Pallas kernels, per_device(): pl.pallas_call(functools.partial(kernel, n_dp, n_mp), out_shape=(jax.Shap...  41.9 us
    unnamed x11, local copies, waits for them, and re-layouts  6.08 us

profile of v1, /device:TPU:0, one launch (start us, length us, event | category | flops | bytes accessed | tf_op | source)
XLA Modules:
  0.0 50.4 jit_solution(15570029378765709002)
XLA Ops:
  0.6 0.0 copy-start
  0.6 1.6 %copy-done = bf16[1024,1024]{1,0:T(8,128)(2,1)S(1)} copy-done((bf16[1024,1024]{1,0:T(8,128)(2,1)S(1)}, bf16[1024,1024]{1,0:T(8,128)(2,1)}, u32[]{:S(2)}) %copy-start) | copy-done | bytes 2097176
  2.2 0.0 copy-start.1
  2.2 1.2 %copy-done.1 = bf16[2048,256]{1,0:T(8,128)(2,1)S(1)} copy-done((bf16[2048,256]{1,0:T(8,128)(2,1)S(1)}, bf16[2048,256]{1,0:T(8,128)(2,1)}, u32[]{:S(2)}) %copy-start.1) | copy-done | bytes 1048600
  3.4 0.0 copy-start.2
  3.5 0.7 %copy-done.2 = s32[2048]{0:T(1024)S(1)} copy-done((s32[2048]{0:T(1024)S(1)}, s32[2048]{0:T(1024)}, u32[]{:S(2)}) %copy-start.2) | copy-done | bytes 8216
  4.1 0.0 copy-start.3
  4.1 0.7 %copy-done.3 = f32[2048]{0:T(1024)S(1)} copy-done((f32[2048]{0:T(1024)S(1)}, f32[2048]{0:T(1024)}, u32[]{:S(2)}) %copy-start.3) | copy-done | bytes 8216
  4.8 41.9 %shard_map.75 = (f32[16,128]{1,0:T(8,128)S(1)}, bf16[512,256]{1,0:T(8,128)(2,1)S(1)}, f32[4,128]{1,0:T(4,128)S(1)}, f32[1,1]{1,0:T(1,128)}) custom-call(s32[16,128]{1,0:T(8,128)S(1)} %bitcast.5, f32[16,128]{1,0:T(8,128)S(1)} %bitcast.6, bf16[2048,256]{1,0:T(8,128)(2,1)S(1)} %copy-done.1, bf16[1024,1024]{1,0:T(8,128)(2,1)S(1)} %copy-done), custom_call_target="tpu_custom_call" | custom-call | tf_op jit(solution)/shard_map/pallas_call | solution.py:293
  46.8 0.6 %copy.12 = f32[2048]{0:T(1024)} copy(f32[2048]{0:T(1024)S(1)} %bitcast.7) | data formatting | bytes 16384
  47.4 0.7 %copy.13 = bf16[512,256]{1,0:T(8,128)(2,1)} copy(bf16[512,256]{1,0:T(8,128)(2,1)S(1)} %get-tuple-element.17) | data formatting | bytes 524288
  48.1 0.6 %copy.14 = f32[512]{0:T(512)} copy(f32[512]{0:T(512)S(1)} %bitcast.8) | data formatting | bytes 4096
Async XLA Ops:
  0.6 1.6 %copy-start = (bf16[1024,1024]{1,0:T(8,128)(2,1)S(1)}, bf16[1024,1024]{1,0:T(8,128)(2,1)}, u32[]{:S(2)}) copy-start(bf16[1024,1024]{1,0:T(8,128)(2,1)} %cents_ref.1) | copy-start | bytes 6291460
  2.2 1.2 %copy-start.1 = (bf16[2048,256]{1,0:T(8,128)(2,1)S(1)}, bf16[2048,256]{1,0:T(8,128)(2,1)}, u32[]{:S(2)}) copy-start(bf16[2048,256]{1,0:T(8,128)(2,1)} %docs_ref.1) | copy-start | bytes 3145732
  3.4 0.7 %copy-start.2 = (s32[2048]{0:T(1024)S(1)}, s32[2048]{0:T(1024)}, u32[]{:S(2)}) copy-start(s32[2048]{0:T(1024)} %param.5) | copy-start | bytes 24580
  4.1 0.7 %copy-start.3 = (f32[2048]{0:T(1024)S(1)}, f32[2048]{0:T(1024)}, u32[]{:S(2)}) copy-start(f32[2048]{0:T(1024)} %param.6) | copy-start | bytes 24580

commit v2 on v1

--- a/solution.py
+++ b/solution.py
@@ -10,13 +10,14 @@
 MESH = pl.DeviceIdType.MESH
 LANES = 128
 CHUNKS = 4
+PARTS = 2
 
 
 def kernel(
-    n_dp, n_mp, assign_ref, quality_ref, docs_ref, cents_ref,
+    n_dp, n_mp, assign_hbm, quality_hbm, docs_hbm, cents_ref,
     dist_ref, new_ref, cq_ref, inertia_ref,
-    fc, acc, acol, own, ysend, ybuf, zsend, zbuf, ag, qg, dbuf, ibuf, isend,
-    a_ss, a_rs, a_ls, g_ss, g_rs, y_ss, y_rs, z_ss, z_rs, d_ss, d_rs, i_ss, i_rs,
+    assign_ref, quality_ref, docs_ref, fc, acc, acol, own, ysend, ybuf, zsend, zbuf, ag, qg, dbuf, ibuf, isend,
+    in_sems, a_ss, a_rs, a_ls, g_ss, g_rs, y_ss, y_rs, z_ss, z_rs, d_ss, d_rs, i_ss, i_rs,
 ):
     f32, bf16 = jnp.float32, jnp.bfloat16
     dp, mp = lax.axis_index("dp"), lax.axis_index("mp")
@@ -27,6 +28,15 @@
     share = new_ref.shape[0]
     nb = rows // LANES
     clen = depth // CHUNKS
+
+    loads = [
+        pltpu.make_async_copy(src, dst, in_sems.at[i])
+        for i, (src, dst) in enumerate(
+            ((assign_hbm, assign_ref), (quality_hbm, quality_ref), (docs_hbm, docs_ref))
+        )
+    ]
+    for load in loads:
+        load.start()
 
     barrier = pltpu.get_barrier_semaphore()
     for s in range(1, n_mp):
@@ -61,6 +71,8 @@
         cents_ref.at[:, pl.ds(pl.multiple_of(mp * width, LANES), width)], fc.at[mp], a_ls
     )
     mine.start()
+    for load in loads:
+        load.wait()
 
     def gather_copies(peer, slot):
         return [
@@ -87,9 +99,13 @@
         weighted = jnp.concatenate(pieces, axis=1)
         return jnp.dot(weighted, docs_ref[...], preferred_element_type=f32)
 
-    def y_copy(h):
-        return pltpu.make_async_remote_copy(
-            src_ref=ysend.at[h], dst_ref=ybuf.at[h], send_sem=y_ss.at[h], recv_sem=y_rs.at[h],
+    part_rows = share // PARTS
+
+    def y_copy(h, p):
+        at = pl.ds(pl.multiple_of(p * part_rows, part_rows), part_rows)
+        return pltpu.make_async_remote_copy(
+            src_ref=ysend.at[h, at], dst_ref=ybuf.at[h, at],
+            send_sem=y_ss.at[h, p], recv_sem=y_rs.at[h, p],
             device_id={"dp": hi * 2 + 1 - lo}, device_id_type=MESH,
         )
 
@@ -97,24 +113,28 @@
     def _(k):
         h = (hi + 1 + k) % n_hi
         ysend[h] = partial(h * 2 + 1 - lo).astype(bf16)
-        y_copy(h).start()
+        for p in range(PARTS):
+            y_copy(h, p).start()
 
     @pl.loop(0, n_hi)
     def _(k):
         h = (hi + 1 + k) % n_hi
         own[h] = partial(h * 2 + lo)
 
-    def z_copy(h, slot):
-        return pltpu.make_async_remote_copy(
-            src_ref=zsend.at[h], dst_ref=zbuf.at[slot], send_sem=z_ss.at[h], recv_sem=z_rs.at[slot],
+    def z_copy(h, slot, p):
+        at = pl.ds(pl.multiple_of(p * part_rows, part_rows), part_rows)
+        return pltpu.make_async_remote_copy(
+            src_ref=zsend.at[h, at], dst_ref=zbuf.at[slot, at],
+            send_sem=z_ss.at[h, p], recv_sem=z_rs.at[slot, p],
             device_id={"dp": h * 2 + lo}, device_id_type=MESH,
         )
 
-    def forward(k):
-        h = (hi + 1 + k) % n_hi
-        y_copy(h).wait_recv()
-        zsend[h] = (own[h] + ybuf[h].astype(f32)).astype(bf16)
-        z_copy(h, hi).start()
+    def forward(t):
+        h, p = (hi + 1 + t // PARTS) % n_hi, t % PARTS
+        at = pl.ds(pl.multiple_of(p * part_rows, part_rows), part_rows)
+        y_copy(h, p).wait_recv()
+        zsend[h, at, :] = (own[h, at, :] + ybuf[h, at, :].astype(f32)).astype(bf16)
+        z_copy(h, hi, p).start()
 
     for b in range(nb):
         ids = jnp.broadcast_to(assign_ref[pl.ds(b, 1), :].astype(f32), (LANES, LANES))
@@ -143,13 +163,13 @@
 
     mine.wait()
     pick(mp, 0, depth, first=True)
-    forwards = n_hi - 1
-    cut = [forwards * c // (CHUNKS - 1) for c in range(CHUNKS)]
-    if CHUNKS > 1:
-        pl.loop(cut[0], cut[1])(forward)
+    forwards = (n_hi - 1) * PARTS
+    cut = [forwards * c // 6 for c in (0, 1, 2, 3, 5, 6)]
+    pl.loop(cut[0], cut[1])(forward)
     for c in range(CHUNKS):
         cent_copy(near, near, c).wait_recv()
     pick(near, 0, depth)
+    pl.loop(cut[1], cut[2])(forward)
 
     lane_len = min(LANES, share)
     groups = share // lane_len
@@ -184,13 +204,14 @@
     totals = lax.fori_loop(0, n_dp, count, jnp.zeros((2 * half, lane_len), f32))
     counts, mass = totals[:groups], totals[half : half + groups]
     cq_ref[...] = mass / (counts + 1.0)
+    pl.loop(cut[2], cut[3])(forward)
 
     for c in range(CHUNKS):
         for peer in fars:
             cent_copy(peer, peer, c).wait_recv()
             pick(peer, c * clen, clen)
-        if c + 2 < CHUNKS:
-            pl.loop(cut[c + 1], cut[c + 2])(forward)
+        if c < 2:
+            pl.loop(cut[c + 3], cut[c + 4])(forward)
 
     @pl.loop(0, nb)
     def _(b):
@@ -233,13 +254,15 @@
 
     ibuf[dp] = folded
 
-    y_copy(hi).wait_recv()
+    for p in range(PARTS):
+        y_copy(hi, p).wait_recv()
     own[hi] = own[hi] + ybuf[hi].astype(f32)
 
     @pl.loop(1, n_hi)
     def _(s):
         h = (hi + s) % n_hi
-        z_copy(h, h).wait_recv()
+        for p in range(PARTS):
+            z_copy(h, h, p).wait_recv()
         own[hi] = own[hi] + zbuf[h].astype(f32)
 
     first = dp * share
@@ -273,11 +296,13 @@
 
     @pl.loop(0, n_hi)
     def _(h):
-        y_copy(h).wait_send()
+        for p in range(PARTS):
+            y_copy(h, p).wait_send()
 
     @pl.loop(1, n_hi)
     def _(s):
-        z_copy((hi + s) % n_hi, hi).wait_send()
+        for p in range(PARTS):
+            z_copy((hi + s) % n_hi, hi, p).wait_send()
 
 
 def per_device(n_dp, n_mp, documents, assign, quality, centroids):
@@ -298,9 +323,12 @@
             jax.ShapeDtypeStruct((share // lane_len, lane_len), f32),
             jax.ShapeDtypeStruct((1, 1), f32),
         ),
-        in_specs=[vmem, vmem, vmem, pl.BlockSpec(memory_space=pl.ANY)],
+        in_specs=[pl.BlockSpec(memory_space=pltpu.MemorySpace.HBM)] * 4,
         out_specs=(vmem, vmem, vmem, pl.BlockSpec(memory_space=pltpu.SMEM)),
         scratch_shapes=[
+            pltpu.VMEM((nb, LANES), jnp.int32),
+            pltpu.VMEM((nb, LANES), f32),
+            pltpu.VMEM((rows, width), bf16),
             pltpu.VMEM((n_mp, depth, width), bf16),
             pltpu.VMEM((rows, width), f32),
             pltpu.VMEM((rows, LANES), f32),
@@ -314,15 +342,15 @@
             pltpu.VMEM((n_mp, nb, LANES), f32),
             pltpu.VMEM((n_dp, 8, LANES), f32),
             pltpu.VMEM((8, LANES), f32),
-            dma((n_mp, CHUNKS)), dma((n_mp, CHUNKS)), dma,
+            dma((3,)), dma((n_mp, CHUNKS)), dma((n_mp, CHUNKS)), dma,
             dma((2, n_dp)), dma((2, n_dp)),
-            dma((n_hi,)), dma((n_hi,)),
-            dma((n_hi,)), dma((n_hi,)),
+            dma((n_hi, PARTS)), dma((n_hi, PARTS)),
+            dma((n_hi, PARTS)), dma((n_hi, PARTS)),
             dma((n_mp,)), dma((n_mp,)),
             dma((n_dp,)), dma((n_dp,)),
         ],
         compiler_params=pltpu.CompilerParams(
-            collective_id=0, has_side_effects=True, vmem_limit_bytes=48 * 2**20
+            collective_id=0, has_side_effects=True, vmem_limit_bytes=60 * 2**20
         ),
     )(assign.reshape(nb, LANES), quality.reshape(nb, LANES), documents, centroids)
     return dist.reshape(rows), new, cq.reshape(share), inertia.reshape(())

time: 50.7 us -> 48.6 us (0.959)
  local copies, waits for them, and re-layouts: 6.08 us -> 4.22 us
    unnamed x11 -> x3, local copies, waits for them, and re-layouts: 6.08 us -> 4.22 us
where the time goes in v2:
time: 48.6 us; the launch traced here: 48.4 us
  Pallas kernels  41.7 us (86%)
  local copies, waits for them, and re-layouts  4.22 us (9%)
  between operations  2.46 us (5%)
    pallas_call x1, Pallas kernels, per_device(): pl.pallas_call(functools.partial(kernel, n_dp, n_mp), out_shape=(jax.Shap...  41.7 us
    unnamed x3, local copies, waits for them, and re-layouts  4.22 us

profile of v2, /device:TPU:0, one launch (start us, length us, event | category | flops | bytes accessed | tf_op | source)
XLA Modules:
  0.0 48.4 jit_solution(5223563945509777400)
XLA Ops:
  0.6 41.7 %shard_map.75 = (f32[16,128]{1,0:T(8,128)}, bf16[512,256]{1,0:T(8,128)(2,1)}, f32[4,128]{1,0:T(4,128)}, f32[1,1]{1,0:T(1,128)}) custom-call(s32[16,128]{1,0:T(8,128)} %bitcast.5, f32[16,128]{1,0:T(8,128)} %bitcast.6, bf16[2048,256]{1,0:T(8,128)(2,1)} %docs_hbm.1, bf16[1024,1024]{1,0:T(8,128)(2,1)} %cents_ref.1), custom_call_target="tpu_custom_call" | custom-call | tf_op jit(solution)/shard_map/pallas_call | solution.py:318
  42.3 1.3 %copy.12 = f32[2048]{0:T(1024)} copy(f32[2048]{0:T(1024)} %bitcast.7) | data formatting | bytes 16384
  43.6 1.7 %copy.13 = bf16[512,256]{1,0:T(8,128)(2,1)} copy(bf16[512,256]{1,0:T(8,128)(2,1)} %get-tuple-element.17) | data formatting | bytes 524288
  45.3 1.3 %copy.14 = f32[512]{0:T(512)} copy(f32[512]{0:T(512)} %bitcast.8) | data formatting | bytes 4096
